TPU v7x, 32 devices: a whole 2x2x4 slice. The times are simulated.
32 devices in a mesh: gx: 8 (over y, x, core), gy: 4 (over z).
Axes of the slice: x: 2, y: 2, z: 4, core: 2. Of those that a mesh axis runs over, the one named last changes fastest.
Arguments:
- signals: float32 [16, 32, 16, 128], P('gx', 'gy'), may hold values from -6 to 6
- tiles: bfloat16 [16, 32, 4, 128, 128], P('gx', 'gy'), may hold values from 0 to 0.00390625
- tile_dir: int32 [16, 32, 4], P('gx', 'gy'), may hold values from 0 to 8
- tile_mask: int32 [16, 32, 4], P('gx', 'gy'), may hold values 0 or 1
- live_rows: int32 [16, 32], P('gx', 'gy'), may hold values from 32 to 128
- bound_rows: int32 [16, 32], P('gx', 'gy'), may hold values from 1 to 32, as said below
- scale_coeffs: float32 [6, 5], replicated, may hold values from -1 to 1
- spectral_bound: float32 [1], replicated, may hold values from 2.5 to 4
Outputs:
- coefficients: float32 [6, 16, 32, 16, 128], P(None, 'gx', 'gy')
- energy: float32 [6, 16], replicated
Inputs may be any that keep to these rules, and one draw needn't show every extreme that they name: `bound_rows`: in every draw, some blocks on every device have exactly 32 boundary rows.
All inputs are finite; a program needn't handle non-finite values. No bound on the sum of `tile_mask` on one device may be relied on, other than what follows from the above.
Results may differ from a plain program's by a relative error of at most 0.0003.
Values may be sent and summed in bfloat16 or wider, within the bound.
A program may use at most 64 MiB of HBM per device.

v0:
```python
import jax
import jax.numpy as jnp
from jax import lax
from jax.sharding import PartitionSpec as P

DEG = 4


def with_halo(array, sides, width):
    for axis, dim in sides:
        devices, length = (lax.axis_size(axis), array.shape[dim])
        up = [(i, (i + 1) % devices) for i in range(devices - 1)]
        down = [(j, i) for i, j in up]
        last = lax.slice_in_dim(array, length - width, length, axis=dim)
        first = lax.slice_in_dim(array, 0, width, axis=dim)
        before = lax.ppermute(last, axis, up)
        after = lax.ppermute(first, axis, down)
        array = jnp.concatenate([before, array, after], axis=dim)
    return array


def scaled_laplacian(values, adjacent, degree, factor):
    return factor * (degree * values - adjacent) - values


def shards(
    signals, tiles, tile_dir, tile_mask, live_rows, bound_rows, scale_coeffs, spectral_bound
):
    tile_size = signals.shape[3]
    extent_x = signals.shape[0]
    extent_y = signals.shape[1]
    slot_count = tiles.shape[2]
    block_count = extent_x * extent_y
    positions = lax.broadcasted_iota(jnp.int32, (1, 1, tile_size), 2)
    live_ind = (positions < live_rows[:, :, None]).astype(jnp.float32)
    bound_ind = (positions < bound_rows[:, :, None]).astype(jnp.float32)
    flat_tiles = tiles.reshape(block_count, slot_count, tile_size, tile_size)

    def adjacency(values):
        own_rows = values.astype(jnp.bfloat16)
        edge_rows = (values * bound_ind[:, :, None, :]).astype(jnp.bfloat16)
        padded = with_halo(edge_rows, (("gx", 0), ("gy", 1)), 1)
        slot_list = []
        for slot_index in range(slot_count):
            picked = jnp.zeros_like(own_rows)
            for direction in range(9):
                step_x = direction // 3 - 1
                step_y = direction % 3 - 1
                if direction == 4:
                    source = own_rows
                else:
                    source = padded[
                        1 + step_x : 1 + step_x + extent_x, 1 + step_y : 1 + step_y + extent_y
                    ]
                matches = (tile_dir[:, :, slot_index] == direction)[:, :, None, None]
                picked = jnp.where(matches, source, picked)
            kept = (tile_mask[:, :, slot_index] == 1)[:, :, None, None]
            picked = jnp.where(kept, picked, jnp.zeros_like(picked))
            slot_list.append(picked)
        inputs = jnp.stack(slot_list, axis=1 + 1)
        flat_inputs = inputs.reshape(block_count, slot_count, inputs.shape[3], tile_size)
        product = lax.dot_general(
            flat_inputs,
            flat_tiles,
            (((1, 3), (1, 3)), ((0,), (0,))),
            preferred_element_type=jnp.float32,
        )
        product = product.reshape(extent_x, extent_y, inputs.shape[3], tile_size)
        return product * live_ind[:, :, None, :]

    channels = signals.shape[2]
    initial = signals * live_ind[:, :, None, :]
    joined = jnp.concatenate([initial, live_ind[:, :, None, :]], axis=2)
    first_pass = adjacency(joined)
    degree = first_pass[:, :, channels:, :]
    factor = 2.0 / spectral_bound[0]
    previous = initial
    current = scaled_laplacian(initial, first_pass[:, :, :channels, :], degree, factor)
    totals = 0.5 * scale_coeffs[:, 0][:, None, None, None, None] * initial[None]
    totals = totals + scale_coeffs[:, 1][:, None, None, None, None] * current[None]
    for degree_index in range(2, DEG + 1):
        adjacent = adjacency(current)
        following = 2.0 * scaled_laplacian(current, adjacent, degree, factor) - previous
        previous = current
        current = following
        totals = totals + scale_coeffs[:, degree_index][:, None, None, None, None] * current[None]
    nodes = extent_x * extent_y * tile_size * lax.axis_size("gx") * lax.axis_size("gy")
    local_sums = jnp.sum(totals * totals, axis=(1, 2, 4))
    energy = lax.psum(local_sums, ("gx", "gy")) / nodes
    return (totals, energy)


def solution(mesh):
    placed = (
        P("gx", "gy", None, None),
        P("gx", "gy", None, None, None),
        P("gx", "gy", None),
        P("gx", "gy", None),
        P("gx", "gy"),
        P("gx", "gy"),
        P(),
        P(),
    )
    return jax.shard_map(
        shards,
        mesh=mesh,
        in_specs=placed,
        out_specs=(P(None, "gx", "gy", None, None), P()),
        check_vma=False,
    )
```

profile of v0, /device:TPU:0, one launch (start us, length us, event | category | flops | bytes accessed | tf_op | source)
XLA Modules:
  0.0 117.8 jit_solution(2510925606802948596)
XLA Ops:
  0.6 0.9 compare_convert_fusion
  1.6 0.8 fusion.35
  2.3 0.9 broadcast_multiply_fusion.1
  3.3 2.4 %collective-permute-start = (bf16[1,8,17,128]{3,2,1,0:T(8,128)(2,1)S(1)}, bf16[1,8,17,128]{3,2,1,0:T(8,128)(2,1)S(1)}, u32[]{:S(2)}, u32[]{:S(2)}) collective-permute-start(bf16[1,8,17,128]{3,2,1,0:T(8,128)(2,1)S(1)} %get-tuple-element.37), channel_id=1, source_target_pairs={{0,4},{4,8},{8,12},{12,16},{16,20},{20,24},{24,28},{1,5},{5,9},{9,... | collective-permute-start | bytes 104456 | tf_op jit(solution)/shard_map/ppermute | solution.py:16
  5.7 1.3 %collective-permute-start.1 = (bf16[1,8,17,128]{3,2,1,0:T(8,128)(2,1)S(1)}, bf16[1,8,17,128]{3,2,1,0:T(8,128)(2,1)S(1)}, u32[]{:S(2)}, u32[]{:S(2)}) collective-permute-start(bf16[1,8,17,128]{3,2,1,0:T(8,128)(2,1)S(1)} %get-tuple-element.38), channel_id=1, source_target_pairs={{4,0},{8,4},{12,8},{16,12},{20,16},{24,20},{28,24},{5,1},{9,5},{13... | collective-permute-start | bytes 104456 | tf_op jit(solution)/shard_map/ppermute | solution.py:17
  7.0 0.8 broadcast_compare_fusion.30
  7.8 0.8 broadcast_compare_fusion.31
  8.7 0.8 slice_compare_fusion.3
  9.8 1.1 collective-permute-done.1
  10.9 1.3 %collective-permute-start.2 = (bf16[4,1,17,128]{3,2,1,0:T(8,128)(2,1)S(1)}, bf16[4,1,17,128]{3,2,1,0:T(8,128)(2,1)S(1)}, u32[]{:S(2)}, u32[]{:S(2)}) collective-permute-start(bf16[4,1,17,128]{3,2,1,0:T(8,128)(2,1)S(1)} %get-tuple-element.23), channel_id=1, source_target_pairs={{1,0},{2,1},{3,2},{5,4},{6,5},{7,6},{9,8},{10,9},{11,10},{13,12},{... | collective-permute-start | bytes 52232 | tf_op jit(solution)/shard_map/ppermute | solution.py:17
  12.2 4.5 %collective-permute-start.3 = (bf16[4,1,17,128]{3,2,1,0:T(8,128)(2,1)S(1)}, bf16[4,1,17,128]{3,2,1,0:T(8,128)(2,1)S(1)}, u32[]{:S(2)}, u32[]{:S(2)}) collective-permute-start(bf16[4,1,17,128]{3,2,1,0:T(8,128)(2,1)S(1)} %get-tuple-element.24), channel_id=1, source_target_pairs={{0,1},{1,2},{2,3},{4,5},{5,6},{6,7},{8,9},{9,10},{10,11},{12,13},{... | collective-permute-start | bytes 52232 | tf_op jit(solution)/shard_map/ppermute | solution.py:16
  17.5 0.8 collective-permute-done.3
  20.2 3.6 %collective-permute-start.4 = (bf16[1,8,16,128]{3,2,1,0:T(8,128)(2,1)S(1)}, bf16[1,8,16,128]{3,2,1,0:T(8,128)(2,1)S(1)}, u32[]{:S(2)}, u32[]{:S(2)}) collective-permute-start(bf16[1,8,16,128]{3,2,1,0:T(8,128)(2,1)S(1)} %get-tuple-element.43), channel_id=1, source_target_pairs={{0,4},{4,8},{8,12},{12,16},{16,20},{20,24},{24,28},{1,5},{5,9},{9,... | collective-permute-start | bytes 98312 | tf_op jit(solution)/shard_map/ppermute | solution.py:16
  23.8 1.3 %collective-permute-start.5 = (bf16[1,8,16,128]{3,2,1,0:T(8,128)(2,1)S(1)}, bf16[1,8,16,128]{3,2,1,0:T(8,128)(2,1)S(1)}, u32[]{:S(2)}, u32[]{:S(2)}) collective-permute-start(bf16[1,8,16,128]{3,2,1,0:T(8,128)(2,1)S(1)} %get-tuple-element.44), channel_id=1, source_target_pairs={{4,0},{8,4},{12,8},{16,12},{20,16},{24,20},{28,24},{5,1},{9,5},{13... | collective-permute-start | bytes 98312 | tf_op jit(solution)/shard_map/ppermute | solution.py:17
  25.1 3.5 %collective-permute-done.5 = bf16[1,8,16,128]{3,2,1,0:T(8,128)(2,1)S(1)} collective-permute-done((bf16[1,8,16,128]{3,2,1,0:T(8,128)(2,1)S(1)}, bf16[1,8,16,128]{3,2,1,0:T(8,128)(2,1)S(1)}, u32[]{:S(2)}, u32[]{:S(2)}) %collective-permute-start.5) | collective-permute-done | bytes 32800 | tf_op jit(solution)/shard_map/ppermute | solution.py:17
  28.6 1.3 %collective-permute-start.6 = (bf16[4,1,16,128]{3,2,1,0:T(8,128)(2,1)S(1)}, bf16[4,1,16,128]{3,2,1,0:T(8,128)(2,1)S(1)}, u32[]{:S(2)}, u32[]{:S(2)}) collective-permute-start(bf16[4,1,16,128]{3,2,1,0:T(8,128)(2,1)S(1)} %get-tuple-element.35), channel_id=1, source_target_pairs={{1,0},{2,1},{3,2},{5,4},{6,5},{7,6},{9,8},{10,9},{11,10},{13,12},{... | collective-permute-start | bytes 49160 | tf_op jit(solution)/shard_map/ppermute | solution.py:17
  29.9 4.9 %collective-permute-start.7 = (bf16[4,1,16,128]{3,2,1,0:T(8,128)(2,1)S(1)}, bf16[4,1,16,128]{3,2,1,0:T(8,128)(2,1)S(1)}, u32[]{:S(2)}, u32[]{:S(2)}) collective-permute-start(bf16[4,1,16,128]{3,2,1,0:T(8,128)(2,1)S(1)} %get-tuple-element.36), channel_id=1, source_target_pairs={{0,1},{1,2},{2,3},{4,5},{5,6},{6,7},{8,9},{9,10},{10,11},{12,13},{... | collective-permute-start | bytes 49160 | tf_op jit(solution)/shard_map/ppermute | solution.py:16
  34.8 1.4 %collective-permute-done.7 = bf16[4,1,16,128]{3,2,1,0:T(8,128)(2,1)S(1)} collective-permute-done((bf16[4,1,16,128]{3,2,1,0:T(8,128)(2,1)S(1)}, bf16[4,1,16,128]{3,2,1,0:T(8,128)(2,1)S(1)}, u32[]{:S(2)}, u32[]{:S(2)}) %collective-permute-start.7) | collective-permute-done | bytes 16416 | tf_op jit(solution)/shard_map/ppermute | solution.py:16
  38.0 3.7 %collective-permute-start.8 = (bf16[1,8,16,128]{3,2,1,0:T(8,128)(2,1)S(1)}, bf16[1,8,16,128]{3,2,1,0:T(8,128)(2,1)S(1)}, u32[]{:S(2)}, u32[]{:S(2)}) collective-permute-start(bf16[1,8,16,128]{3,2,1,0:T(8,128)(2,1)S(1)} %get-tuple-element.41), channel_id=1, source_target_pairs={{0,4},{4,8},{8,12},{12,16},{16,20},{20,24},{24,28},{1,5},{5,9},{9,... | collective-permute-start | bytes 98312 | tf_op jit(solution)/shard_map/ppermute | solution.py:16
  41.7 1.3 %collective-permute-start.9 = (bf16[1,8,16,128]{3,2,1,0:T(8,128)(2,1)S(1)}, bf16[1,8,16,128]{3,2,1,0:T(8,128)(2,1)S(1)}, u32[]{:S(2)}, u32[]{:S(2)}) collective-permute-start(bf16[1,8,16,128]{3,2,1,0:T(8,128)(2,1)S(1)} %get-tuple-element.42), channel_id=1, source_target_pairs={{4,0},{8,4},{12,8},{16,12},{20,16},{24,20},{28,24},{5,1},{9,5},{13... | collective-permute-start | bytes 98312 | tf_op jit(solution)/shard_map/ppermute | solution.py:17
  43.0 2.2 %collective-permute-done.9 = bf16[1,8,16,128]{3,2,1,0:T(8,128)(2,1)S(1)} collective-permute-done((bf16[1,8,16,128]{3,2,1,0:T(8,128)(2,1)S(1)}, bf16[1,8,16,128]{3,2,1,0:T(8,128)(2,1)S(1)}, u32[]{:S(2)}, u32[]{:S(2)}) %collective-permute-start.9) | collective-permute-done | bytes 32800 | tf_op jit(solution)/shard_map/ppermute | solution.py:17
  45.2 1.3 %collective-permute-start.10 = (bf16[4,1,16,128]{3,2,1,0:T(8,128)(2,1)S(1)}, bf16[4,1,16,128]{3,2,1,0:T(8,128)(2,1)S(1)}, u32[]{:S(2)}, u32[]{:S(2)}) collective-permute-start(bf16[4,1,16,128]{3,2,1,0:T(8,128)(2,1)S(1)} %get-tuple-element.31), channel_id=1, source_target_pairs={{1,0},{2,1},{3,2},{5,4},{6,5},{7,6},{9,8},{10,9},{11,10},{13,12},{... | collective-permute-start | bytes 49160 | tf_op jit(solution)/shard_map/ppermute | solution.py:17
  46.4 4.8 %collective-permute-start.11 = (bf16[4,1,16,128]{3,2,1,0:T(8,128)(2,1)S(1)}, bf16[4,1,16,128]{3,2,1,0:T(8,128)(2,1)S(1)}, u32[]{:S(2)}, u32[]{:S(2)}) collective-permute-start(bf16[4,1,16,128]{3,2,1,0:T(8,128)(2,1)S(1)} %get-tuple-element.32), channel_id=1, source_target_pairs={{0,1},{1,2},{2,3},{4,5},{5,6},{6,7},{8,9},{9,10},{10,11},{12,13},{... | collective-permute-start | bytes 49160 | tf_op jit(solution)/shard_map/ppermute | solution.py:16
  51.3 1.4 %collective-permute-done.11 = bf16[4,1,16,128]{3,2,1,0:T(8,128)(2,1)S(1)} collective-permute-done((bf16[4,1,16,128]{3,2,1,0:T(8,128)(2,1)S(1)}, bf16[4,1,16,128]{3,2,1,0:T(8,128)(2,1)S(1)}, u32[]{:S(2)}, u32[]{:S(2)}) %collective-permute-start.11) | collective-permute-done | bytes 16416 | tf_op jit(solution)/shard_map/ppermute | solution.py:16
  54.5 4.1 %collective-permute-start.12 = (bf16[1,8,16,128]{3,2,1,0:T(8,128)(2,1)S(1)}, bf16[1,8,16,128]{3,2,1,0:T(8,128)(2,1)S(1)}, u32[]{:S(2)}, u32[]{:S(2)}) collective-permute-start(bf16[1,8,16,128]{3,2,1,0:T(8,128)(2,1)S(1)} %get-tuple-element.39), channel_id=1, source_target_pairs={{0,4},{4,8},{8,12},{12,16},{16,20},{20,24},{24,28},{1,5},{5,9},{9,... | collective-permute-start | bytes 98312 | tf_op jit(solution)/shard_map/ppermute | solution.py:16
  58.6 1.3 %collective-permute-start.13 = (bf16[1,8,16,128]{3,2,1,0:T(8,128)(2,1)S(1)}, bf16[1,8,16,128]{3,2,1,0:T(8,128)(2,1)S(1)}, u32[]{:S(2)}, u32[]{:S(2)}) collective-permute-start(bf16[1,8,16,128]{3,2,1,0:T(8,128)(2,1)S(1)} %get-tuple-element.40), channel_id=1, source_target_pairs={{4,0},{8,4},{12,8},{16,12},{20,16},{24,20},{28,24},{5,1},{9,5},{13... | collective-permute-start | bytes 98312 | tf_op jit(solution)/shard_map/ppermute | solution.py:17
  59.9 2.4 %collective-permute-done.13 = bf16[1,8,16,128]{3,2,1,0:T(8,128)(2,1)S(1)} collective-permute-done((bf16[1,8,16,128]{3,2,1,0:T(8,128)(2,1)S(1)}, bf16[1,8,16,128]{3,2,1,0:T(8,128)(2,1)S(1)}, u32[]{:S(2)}, u32[]{:S(2)}) %collective-permute-start.13) | collective-permute-done | bytes 32800 | tf_op jit(solution)/shard_map/ppermute | solution.py:17
  62.4 1.3 %collective-permute-start.14 = (bf16[4,1,16,128]{3,2,1,0:T(8,128)(2,1)S(1)}, bf16[4,1,16,128]{3,2,1,0:T(8,128)(2,1)S(1)}, u32[]{:S(2)}, u32[]{:S(2)}) collective-permute-start(bf16[4,1,16,128]{3,2,1,0:T(8,128)(2,1)S(1)} %get-tuple-element.27), channel_id=1, source_target_pairs={{1,0},{2,1},{3,2},{5,4},{6,5},{7,6},{9,8},{10,9},{11,10},{13,12},{... | collective-permute-start | bytes 49160 | tf_op jit(solution)/shard_map/ppermute | solution.py:17
  63.6 4.8 %collective-permute-start.15 = (bf16[4,1,16,128]{3,2,1,0:T(8,128)(2,1)S(1)}, bf16[4,1,16,128]{3,2,1,0:T(8,128)(2,1)S(1)}, u32[]{:S(2)}, u32[]{:S(2)}) collective-permute-start(bf16[4,1,16,128]{3,2,1,0:T(8,128)(2,1)S(1)} %get-tuple-element.28), channel_id=1, source_target_pairs={{0,1},{1,2},{2,3},{4,5},{5,6},{6,7},{8,9},{9,10},{10,11},{12,13},{... | collective-permute-start | bytes 49160 | tf_op jit(solution)/shard_map/ppermute | solution.py:16
  68.7 1.2 %collective-permute-done.15 = bf16[4,1,16,128]{3,2,1,0:T(8,128)(2,1)S(1)} collective-permute-done((bf16[4,1,16,128]{3,2,1,0:T(8,128)(2,1)S(1)}, bf16[4,1,16,128]{3,2,1,0:T(8,128)(2,1)S(1)}, u32[]{:S(2)}, u32[]{:S(2)}) %collective-permute-start.15) | collective-permute-done | bytes 16416 | tf_op jit(solution)/shard_map/ppermute | solution.py:16
  71.6 1.3 %multiply_reduce_fusion = (f32[6,16]{1,0:T(8,128)S(1)}, f32[6,2,8,16,128]{4,3,2,1,0:T(8,128)}) fusion(f32[2,8,16,128]{3,2,1,0:T(8,128)S(1)} %multiply_subtract_fusion, f32[6]{0:T(128)S(1)} %get-tuple-element.5, f32[2,8,16,128]{3,2,1,0:T(8,128)S(1)} %get-tuple-element.12, f32[6]{0:T(128)S(1)} %get-tuple-element.6, f32[2,8,16,128]{3,2,1,0:T(8,128)S(1)} %get-tuple-element.16, ...), kind=kLoop, calls=%fused_computation | loop fusion | flops 2162592 | bytes 1442296 | tf_op jit(solution)/shard_map/reduce_sum | solution.py:88
  72.9 44.3 %psum.7 = f32[6,16]{1,0:T(8,128)S(1)} all-reduce(f32[6,16]{1,0:T(8,128)S(1)} %get-tuple-element.7), channel_id=1, replica_groups=mesh['gx'=8,'gy'=4] {'gx','gy'}, use_global_device_ids=true, to_apply=%region_1.2 | all-reduce | flops 96 | bytes 768 | tf_op jit(solution)/shard_map/psum | solution.py:89
  (76 shorter events, 8.0 us)
Async XLA Ops:
  0.6 18.8 %copy-start = (bf16[2,8,4,128,128]{4,3,2,1,0:T(8,128)(2,1)S(1)}, bf16[2,8,4,128,128]{4,3,2,1,0:T(8,128)(2,1)}, u32[]{:S(2)}) copy-start(bf16[2,8,4,128,128]{4,3,2,1,0:T(8,128)(2,1)} %param.9) | copy-start | bytes 6291460
  3.3 6.5 %collective-permute-start = (bf16[1,8,17,128]{3,2,1,0:T(8,128)(2,1)S(1)}, bf16[1,8,17,128]{3,2,1,0:T(8,128)(2,1)S(1)}, u32[]{:S(2)}, u32[]{:S(2)}) collective-permute-start(bf16[1,8,17,128]{3,2,1,0:T(8,128)(2,1)S(1)} %get-tuple-element.37), channel_id=1, source_target_pairs={{0,4},{4,8},{8,12},{12,16},{16,20},{20,24},{24,28},{1,5},{5,9},{9,... | collective-permute-start | bytes 104456 | tf_op jit(solution)/shard_map/ppermute | solution.py:16
  5.7 5.2 %collective-permute-start.1 = (bf16[1,8,17,128]{3,2,1,0:T(8,128)(2,1)S(1)}, bf16[1,8,17,128]{3,2,1,0:T(8,128)(2,1)S(1)}, u32[]{:S(2)}, u32[]{:S(2)}) collective-permute-start(bf16[1,8,17,128]{3,2,1,0:T(8,128)(2,1)S(1)} %get-tuple-element.38), channel_id=1, source_target_pairs={{4,0},{8,4},{12,8},{16,12},{20,16},{24,20},{28,24},{5,1},{9,5},{13... | collective-permute-start | bytes 104456 | tf_op jit(solution)/shard_map/ppermute | solution.py:17
  10.9 6.6 %collective-permute-start.2 = (bf16[4,1,17,128]{3,2,1,0:T(8,128)(2,1)S(1)}, bf16[4,1,17,128]{3,2,1,0:T(8,128)(2,1)S(1)}, u32[]{:S(2)}, u32[]{:S(2)}) collective-permute-start(bf16[4,1,17,128]{3,2,1,0:T(8,128)(2,1)S(1)} %get-tuple-element.23), channel_id=1, source_target_pairs={{1,0},{2,1},{3,2},{5,4},{6,5},{7,6},{9,8},{10,9},{11,10},{13,12},{... | collective-permute-start | bytes 52232 | tf_op jit(solution)/shard_map/ppermute | solution.py:17
  12.2 6.1 %collective-permute-start.3 = (bf16[4,1,17,128]{3,2,1,0:T(8,128)(2,1)S(1)}, bf16[4,1,17,128]{3,2,1,0:T(8,128)(2,1)S(1)}, u32[]{:S(2)}, u32[]{:S(2)}) collective-permute-start(bf16[4,1,17,128]{3,2,1,0:T(8,128)(2,1)S(1)} %get-tuple-element.24), channel_id=1, source_target_pairs={{0,1},{1,2},{2,3},{4,5},{5,6},{6,7},{8,9},{9,10},{10,11},{12,13},{... | collective-permute-start | bytes 52232 | tf_op jit(solution)/shard_map/ppermute | solution.py:16
  19.2 1.0 copy-start.1
  20.2 4.9 %collective-permute-start.4 = (bf16[1,8,16,128]{3,2,1,0:T(8,128)(2,1)S(1)}, bf16[1,8,16,128]{3,2,1,0:T(8,128)(2,1)S(1)}, u32[]{:S(2)}, u32[]{:S(2)}) collective-permute-start(bf16[1,8,16,128]{3,2,1,0:T(8,128)(2,1)S(1)} %get-tuple-element.43), channel_id=1, source_target_pairs={{0,4},{4,8},{8,12},{12,16},{16,20},{20,24},{24,28},{1,5},{5,9},{9,... | collective-permute-start | bytes 98312 | tf_op jit(solution)/shard_map/ppermute | solution.py:16
  23.8 4.8 %collective-permute-start.5 = (bf16[1,8,16,128]{3,2,1,0:T(8,128)(2,1)S(1)}, bf16[1,8,16,128]{3,2,1,0:T(8,128)(2,1)S(1)}, u32[]{:S(2)}, u32[]{:S(2)}) collective-permute-start(bf16[1,8,16,128]{3,2,1,0:T(8,128)(2,1)S(1)} %get-tuple-element.44), channel_id=1, source_target_pairs={{4,0},{8,4},{12,8},{16,12},{20,16},{24,20},{28,24},{5,1},{9,5},{13... | collective-permute-start | bytes 98312 | tf_op jit(solution)/shard_map/ppermute | solution.py:17
  28.6 6.2 %collective-permute-start.6 = (bf16[4,1,16,128]{3,2,1,0:T(8,128)(2,1)S(1)}, bf16[4,1,16,128]{3,2,1,0:T(8,128)(2,1)S(1)}, u32[]{:S(2)}, u32[]{:S(2)}) collective-permute-start(bf16[4,1,16,128]{3,2,1,0:T(8,128)(2,1)S(1)} %get-tuple-element.35), channel_id=1, source_target_pairs={{1,0},{2,1},{3,2},{5,4},{6,5},{7,6},{9,8},{10,9},{11,10},{13,12},{... | collective-permute-start | bytes 49160 | tf_op jit(solution)/shard_map/ppermute | solution.py:17
  29.9 6.3 %collective-permute-start.7 = (bf16[4,1,16,128]{3,2,1,0:T(8,128)(2,1)S(1)}, bf16[4,1,16,128]{3,2,1,0:T(8,128)(2,1)S(1)}, u32[]{:S(2)}, u32[]{:S(2)}) collective-permute-start(bf16[4,1,16,128]{3,2,1,0:T(8,128)(2,1)S(1)} %get-tuple-element.36), channel_id=1, source_target_pairs={{0,1},{1,2},{2,3},{4,5},{5,6},{6,7},{8,9},{9,10},{10,11},{12,13},{... | collective-permute-start | bytes 49160 | tf_op jit(solution)/shard_map/ppermute | solution.py:16
  38.0 5.0 %collective-permute-start.8 = (bf16[1,8,16,128]{3,2,1,0:T(8,128)(2,1)S(1)}, bf16[1,8,16,128]{3,2,1,0:T(8,128)(2,1)S(1)}, u32[]{:S(2)}, u32[]{:S(2)}) collective-permute-start(bf16[1,8,16,128]{3,2,1,0:T(8,128)(2,1)S(1)} %get-tuple-element.41), channel_id=1, source_target_pairs={{0,4},{4,8},{8,12},{12,16},{16,20},{20,24},{24,28},{1,5},{5,9},{9,... | collective-permute-start | bytes 98312 | tf_op jit(solution)/shard_map/ppermute | solution.py:16
  41.7 3.5 %collective-permute-start.9 = (bf16[1,8,16,128]{3,2,1,0:T(8,128)(2,1)S(1)}, bf16[1,8,16,128]{3,2,1,0:T(8,128)(2,1)S(1)}, u32[]{:S(2)}, u32[]{:S(2)}) collective-permute-start(bf16[1,8,16,128]{3,2,1,0:T(8,128)(2,1)S(1)} %get-tuple-element.42), channel_id=1, source_target_pairs={{4,0},{8,4},{12,8},{16,12},{20,16},{24,20},{28,24},{5,1},{9,5},{13... | collective-permute-start | bytes 98312 | tf_op jit(solution)/shard_map/ppermute | solution.py:17
  45.2 6.1 %collective-permute-start.10 = (bf16[4,1,16,128]{3,2,1,0:T(8,128)(2,1)S(1)}, bf16[4,1,16,128]{3,2,1,0:T(8,128)(2,1)S(1)}, u32[]{:S(2)}, u32[]{:S(2)}) collective-permute-start(bf16[4,1,16,128]{3,2,1,0:T(8,128)(2,1)S(1)} %get-tuple-element.31), channel_id=1, source_target_pairs={{1,0},{2,1},{3,2},{5,4},{6,5},{7,6},{9,8},{10,9},{11,10},{13,12},{... | collective-permute-start | bytes 49160 | tf_op jit(solution)/shard_map/ppermute | solution.py:17
  46.4 6.3 %collective-permute-start.11 = (bf16[4,1,16,128]{3,2,1,0:T(8,128)(2,1)S(1)}, bf16[4,1,16,128]{3,2,1,0:T(8,128)(2,1)S(1)}, u32[]{:S(2)}, u32[]{:S(2)}) collective-permute-start(bf16[4,1,16,128]{3,2,1,0:T(8,128)(2,1)S(1)} %get-tuple-element.32), channel_id=1, source_target_pairs={{0,1},{1,2},{2,3},{4,5},{5,6},{6,7},{8,9},{9,10},{10,11},{12,13},{... | collective-permute-start | bytes 49160 | tf_op jit(solution)/shard_map/ppermute | solution.py:16
  53.5 15.0 %copy-start.2 = (f32[6,5]{1,0:T(8,128)S(1)}, f32[6,5]{1,0:T(8,128)}, u32[]{:S(2)}) copy-start(f32[6,5]{1,0:T(8,128)} %param.14) | copy-start | bytes 364
  54.5 5.4 %collective-permute-start.12 = (bf16[1,8,16,128]{3,2,1,0:T(8,128)(2,1)S(1)}, bf16[1,8,16,128]{3,2,1,0:T(8,128)(2,1)S(1)}, u32[]{:S(2)}, u32[]{:S(2)}) collective-permute-start(bf16[1,8,16,128]{3,2,1,0:T(8,128)(2,1)S(1)} %get-tuple-element.39), channel_id=1, source_target_pairs={{0,4},{4,8},{8,12},{12,16},{16,20},{20,24},{24,28},{1,5},{5,9},{9,... | collective-permute-start | bytes 98312 | tf_op jit(solution)/shard_map/ppermute | solution.py:16
  58.6 3.7 %collective-permute-start.13 = (bf16[1,8,16,128]{3,2,1,0:T(8,128)(2,1)S(1)}, bf16[1,8,16,128]{3,2,1,0:T(8,128)(2,1)S(1)}, u32[]{:S(2)}, u32[]{:S(2)}) collective-permute-start(bf16[1,8,16,128]{3,2,1,0:T(8,128)(2,1)S(1)} %get-tuple-element.40), channel_id=1, source_target_pairs={{4,0},{8,4},{12,8},{16,12},{20,16},{24,20},{28,24},{5,1},{9,5},{13... | collective-permute-start | bytes 98312 | tf_op jit(solution)/shard_map/ppermute | solution.py:17
  62.4 6.4 %collective-permute-start.14 = (bf16[4,1,16,128]{3,2,1,0:T(8,128)(2,1)S(1)}, bf16[4,1,16,128]{3,2,1,0:T(8,128)(2,1)S(1)}, u32[]{:S(2)}, u32[]{:S(2)}) collective-permute-start(bf16[4,1,16,128]{3,2,1,0:T(8,128)(2,1)S(1)} %get-tuple-element.27), channel_id=1, source_target_pairs={{1,0},{2,1},{3,2},{5,4},{6,5},{7,6},{9,8},{10,9},{11,10},{13,12},{... | collective-permute-start | bytes 49160 | tf_op jit(solution)/shard_map/ppermute | solution.py:17
  63.6 6.3 %collective-permute-start.15 = (bf16[4,1,16,128]{3,2,1,0:T(8,128)(2,1)S(1)}, bf16[4,1,16,128]{3,2,1,0:T(8,128)(2,1)S(1)}, u32[]{:S(2)}, u32[]{:S(2)}) collective-permute-start(bf16[4,1,16,128]{3,2,1,0:T(8,128)(2,1)S(1)} %get-tuple-element.28), channel_id=1, source_target_pairs={{0,1},{1,2},{2,3},{4,5},{5,6},{6,7},{8,9},{9,10},{10,11},{12,13},{... | collective-permute-start | bytes 49160 | tf_op jit(solution)/shard_map/ppermute | solution.py:16
where the time goes:
time: 119 us; the launch traced here: 118 us
  blocking collectives  44.3 us (37%)
  starting transfers between devices  43.2 us (36%)
  waiting for transfers between devices  14 us (12%)
  other arithmetic  11.6 us (10%)
  matrix products  2.6 us (2%)
  between operations  1.96 us (2%)
    psum x1, blocking collectives, shards(): energy = lax.psum(local_sums, ('gx', 'gy')) / nodes  44.3 us
    ppermute x8, starting transfers between devices, with_halo(): before = lax.ppermute(last, axis, up)  32.9 us
    ppermute x8, starting transfers between devices, with_halo(): after = lax.ppermute(first, axis, down)  10.3 us
    ppermute x8, waiting for transfers between devices, with_halo(): after = lax.ppermute(first, axis, down)  9.19 us
    ppermute x8, waiting for transfers between devices, with_halo(): before = lax.ppermute(last, axis, up)  4.79 us
    select_n x16, other arithmetic, adjacency(): picked = jnp.where(kept, picked, jnp.zeros_like(picked))  3.91 us
    dot_general x4, matrix products, adjacency(): lax.dot_general(flat_inputs, flat_tiles, (((1, 3), (1, 3)), ((0,), (0,)))...  2.6 us
  transfers between devices with their start and end apart: 16, of which 8 were waited for; matrix products, arithmetic and copies ran while one was open for 2% of the time, Pallas kernels for 0%

commit v1 on v0

--- a/solution.py
+++ b/solution.py
@@ -86,7 +86,7 @@
         totals = totals + scale_coeffs[:, degree_index][:, None, None, None, None] * current[None]
     nodes = extent_x * extent_y * tile_size * lax.axis_size("gx") * lax.axis_size("gy")
     local_sums = jnp.sum(totals * totals, axis=(1, 2, 4))
-    energy = lax.psum(local_sums, ("gx", "gy")) / nodes
+    energy = lax.psum(lax.psum(local_sums, "gy"), "gx") / nodes
     return (totals, energy)
 
 

time: 119 us -> 102 us (0.86)
  the two profiles are of different devices: /device:TPU:0 before, /device:TPU:5 now
where the time goes in v1:
time: 102 us; the launch traced here: 101 us
  starting transfers between devices  46.1 us (45%)
  blocking collectives  27.8 us (27%)
  other arithmetic  11.6 us (11%)
  waiting for transfers between devices  11 us (11%)
  matrix products  2.6 us (3%)
  between operations  1.97 us (2%)
    ppermute x8, starting transfers between devices, with_halo(): before = lax.ppermute(last, axis, up)  31 us
    psum x2, blocking collectives, shards(): energy = lax.psum(lax.psum(local_sums, 'gy'), 'gx') / nodes  27.8 us
    ppermute x8, starting transfers between devices, with_halo(): after = lax.ppermute(first, axis, down)  15.1 us
    ppermute x8, waiting for transfers between devices, with_halo(): after = lax.ppermute(first, axis, down)  8.47 us
    select_n x16, other arithmetic, adjacency(): picked = jnp.where(kept, picked, jnp.zeros_like(picked))  3.91 us
    dot_general x4, matrix products, adjacency(): lax.dot_general(flat_inputs, flat_tiles, (((1, 3), (1, 3)), ((0,), (0,)))...  2.6 us
    ppermute x8, waiting for transfers between devices, with_halo(): before = lax.ppermute(last, axis, up)  2.49 us
  transfers between devices with their start and end apart: 16, of which 8 were waited for; matrix products, arithmetic and copies ran while one was open for 3% of the time, Pallas kernels for 0%

profile of v1, /device:TPU:5, one launch (start us, length us, event | category | flops | bytes accessed | tf_op | source)
XLA Modules:
  0.0 101.2 jit_solution(18064448871456457632)
XLA Ops:
  0.6 0.9 compare_convert_fusion
  1.6 0.8 fusion.35
  2.3 0.9 broadcast_multiply_fusion.1
  3.3 3.7 %collective-permute-start = (bf16[1,8,17,128]{3,2,1,0:T(8,128)(2,1)S(1)}, bf16[1,8,17,128]{3,2,1,0:T(8,128)(2,1)S(1)}, u32[]{:S(2)}, u32[]{:S(2)}) collective-permute-start(bf16[1,8,17,128]{3,2,1,0:T(8,128)(2,1)S(1)} %get-tuple-element.37), channel_id=1, source_target_pairs={{0,4},{4,8},{8,12},{12,16},{16,20},{20,24},{24,28},{1,5},{5,9},{9,... | collective-permute-start | bytes 104456 | tf_op jit(solution)/shard_map/ppermute | solution.py:16
  7.0 1.9 %collective-permute-start.1 = (bf16[1,8,17,128]{3,2,1,0:T(8,128)(2,1)S(1)}, bf16[1,8,17,128]{3,2,1,0:T(8,128)(2,1)S(1)}, u32[]{:S(2)}, u32[]{:S(2)}) collective-permute-start(bf16[1,8,17,128]{3,2,1,0:T(8,128)(2,1)S(1)} %get-tuple-element.38), channel_id=1, source_target_pairs={{4,0},{8,4},{12,8},{16,12},{20,16},{24,20},{28,24},{5,1},{9,5},{13... | collective-permute-start | bytes 104456 | tf_op jit(solution)/shard_map/ppermute | solution.py:17
  8.9 0.8 broadcast_compare_fusion.30
  9.8 0.8 broadcast_compare_fusion.31
  10.6 0.8 slice_compare_fusion.3
  11.7 0.7 collective-permute-done.1
  12.4 1.3 %collective-permute-start.2 = (bf16[4,1,17,128]{3,2,1,0:T(8,128)(2,1)S(1)}, bf16[4,1,17,128]{3,2,1,0:T(8,128)(2,1)S(1)}, u32[]{:S(2)}, u32[]{:S(2)}) collective-permute-start(bf16[4,1,17,128]{3,2,1,0:T(8,128)(2,1)S(1)} %get-tuple-element.23), channel_id=1, source_target_pairs={{1,0},{2,1},{3,2},{5,4},{6,5},{7,6},{9,8},{10,9},{11,10},{13,12},{... | collective-permute-start | bytes 52232 | tf_op jit(solution)/shard_map/ppermute | solution.py:17
  13.7 4.0 %collective-permute-start.3 = (bf16[4,1,17,128]{3,2,1,0:T(8,128)(2,1)S(1)}, bf16[4,1,17,128]{3,2,1,0:T(8,128)(2,1)S(1)}, u32[]{:S(2)}, u32[]{:S(2)}) collective-permute-start(bf16[4,1,17,128]{3,2,1,0:T(8,128)(2,1)S(1)} %get-tuple-element.24), channel_id=1, source_target_pairs={{0,1},{1,2},{2,3},{4,5},{5,6},{6,7},{8,9},{9,10},{10,11},{12,13},{... | collective-permute-start | bytes 52232 | tf_op jit(solution)/shard_map/ppermute | solution.py:16
  19.8 0.7 fusion
  20.6 4.1 %collective-permute-start.4 = (bf16[1,8,16,128]{3,2,1,0:T(8,128)(2,1)S(1)}, bf16[1,8,16,128]{3,2,1,0:T(8,128)(2,1)S(1)}, u32[]{:S(2)}, u32[]{:S(2)}) collective-permute-start(bf16[1,8,16,128]{3,2,1,0:T(8,128)(2,1)S(1)} %get-tuple-element.43), channel_id=1, source_target_pairs={{0,4},{4,8},{8,12},{12,16},{16,20},{20,24},{24,28},{1,5},{5,9},{9,... | collective-permute-start | bytes 98312 | tf_op jit(solution)/shard_map/ppermute | solution.py:16
  24.7 1.9 %collective-permute-start.5 = (bf16[1,8,16,128]{3,2,1,0:T(8,128)(2,1)S(1)}, bf16[1,8,16,128]{3,2,1,0:T(8,128)(2,1)S(1)}, u32[]{:S(2)}, u32[]{:S(2)}) collective-permute-start(bf16[1,8,16,128]{3,2,1,0:T(8,128)(2,1)S(1)} %get-tuple-element.44), channel_id=1, source_target_pairs={{4,0},{8,4},{12,8},{16,12},{20,16},{24,20},{28,24},{5,1},{9,5},{13... | collective-permute-start | bytes 98312 | tf_op jit(solution)/shard_map/ppermute | solution.py:17
  26.6 3.3 %collective-permute-done.5 = bf16[1,8,16,128]{3,2,1,0:T(8,128)(2,1)S(1)} collective-permute-done((bf16[1,8,16,128]{3,2,1,0:T(8,128)(2,1)S(1)}, bf16[1,8,16,128]{3,2,1,0:T(8,128)(2,1)S(1)}, u32[]{:S(2)}, u32[]{:S(2)}) %collective-permute-start.5) | collective-permute-done | bytes 32800 | tf_op jit(solution)/shard_map/ppermute | solution.py:17
  29.9 1.3 %collective-permute-start.6 = (bf16[4,1,16,128]{3,2,1,0:T(8,128)(2,1)S(1)}, bf16[4,1,16,128]{3,2,1,0:T(8,128)(2,1)S(1)}, u32[]{:S(2)}, u32[]{:S(2)}) collective-permute-start(bf16[4,1,16,128]{3,2,1,0:T(8,128)(2,1)S(1)} %get-tuple-element.35), channel_id=1, source_target_pairs={{1,0},{2,1},{3,2},{5,4},{6,5},{7,6},{9,8},{10,9},{11,10},{13,12},{... | collective-permute-start | bytes 49160 | tf_op jit(solution)/shard_map/ppermute | solution.py:17
  31.2 4.6 %collective-permute-start.7 = (bf16[4,1,16,128]{3,2,1,0:T(8,128)(2,1)S(1)}, bf16[4,1,16,128]{3,2,1,0:T(8,128)(2,1)S(1)}, u32[]{:S(2)}, u32[]{:S(2)}) collective-permute-start(bf16[4,1,16,128]{3,2,1,0:T(8,128)(2,1)S(1)} %get-tuple-element.36), channel_id=1, source_target_pairs={{0,1},{1,2},{2,3},{4,5},{5,6},{6,7},{8,9},{9,10},{10,11},{12,13},{... | collective-permute-start | bytes 49160 | tf_op jit(solution)/shard_map/ppermute | solution.py:16
  35.8 0.8 collective-permute-done.7
  38.4 2.8 %collective-permute-start.8 = (bf16[1,8,16,128]{3,2,1,0:T(8,128)(2,1)S(1)}, bf16[1,8,16,128]{3,2,1,0:T(8,128)(2,1)S(1)}, u32[]{:S(2)}, u32[]{:S(2)}) collective-permute-start(bf16[1,8,16,128]{3,2,1,0:T(8,128)(2,1)S(1)} %get-tuple-element.41), channel_id=1, source_target_pairs={{0,4},{4,8},{8,12},{12,16},{16,20},{20,24},{24,28},{1,5},{5,9},{9,... | collective-permute-start | bytes 98312 | tf_op jit(solution)/shard_map/ppermute | solution.py:16
  41.2 2.6 %collective-permute-start.9 = (bf16[1,8,16,128]{3,2,1,0:T(8,128)(2,1)S(1)}, bf16[1,8,16,128]{3,2,1,0:T(8,128)(2,1)S(1)}, u32[]{:S(2)}, u32[]{:S(2)}) collective-permute-start(bf16[1,8,16,128]{3,2,1,0:T(8,128)(2,1)S(1)} %get-tuple-element.42), channel_id=1, source_target_pairs={{4,0},{8,4},{12,8},{16,12},{20,16},{24,20},{28,24},{5,1},{9,5},{13... | collective-permute-start | bytes 98312 | tf_op jit(solution)/shard_map/ppermute | solution.py:17
  43.8 2.6 %collective-permute-done.9 = bf16[1,8,16,128]{3,2,1,0:T(8,128)(2,1)S(1)} collective-permute-done((bf16[1,8,16,128]{3,2,1,0:T(8,128)(2,1)S(1)}, bf16[1,8,16,128]{3,2,1,0:T(8,128)(2,1)S(1)}, u32[]{:S(2)}, u32[]{:S(2)}) %collective-permute-start.9) | collective-permute-done | bytes 32800 | tf_op jit(solution)/shard_map/ppermute | solution.py:17
  46.4 1.3 %collective-permute-start.10 = (bf16[4,1,16,128]{3,2,1,0:T(8,128)(2,1)S(1)}, bf16[4,1,16,128]{3,2,1,0:T(8,128)(2,1)S(1)}, u32[]{:S(2)}, u32[]{:S(2)}) collective-permute-start(bf16[4,1,16,128]{3,2,1,0:T(8,128)(2,1)S(1)} %get-tuple-element.31), channel_id=1, source_target_pairs={{1,0},{2,1},{3,2},{5,4},{6,5},{7,6},{9,8},{10,9},{11,10},{13,12},{... | collective-permute-start | bytes 49160 | tf_op jit(solution)/shard_map/ppermute | solution.py:17
  47.7 4.5 %collective-permute-start.11 = (bf16[4,1,16,128]{3,2,1,0:T(8,128)(2,1)S(1)}, bf16[4,1,16,128]{3,2,1,0:T(8,128)(2,1)S(1)}, u32[]{:S(2)}, u32[]{:S(2)}) collective-permute-start(bf16[4,1,16,128]{3,2,1,0:T(8,128)(2,1)S(1)} %get-tuple-element.32), channel_id=1, source_target_pairs={{0,1},{1,2},{2,3},{4,5},{5,6},{6,7},{8,9},{9,10},{10,11},{12,13},{... | collective-permute-start | bytes 49160 | tf_op jit(solution)/shard_map/ppermute | solution.py:16
  52.3 0.8 collective-permute-done.11
  54.9 2.8 %collective-permute-start.12 = (bf16[1,8,16,128]{3,2,1,0:T(8,128)(2,1)S(1)}, bf16[1,8,16,128]{3,2,1,0:T(8,128)(2,1)S(1)}, u32[]{:S(2)}, u32[]{:S(2)}) collective-permute-start(bf16[1,8,16,128]{3,2,1,0:T(8,128)(2,1)S(1)} %get-tuple-element.39), channel_id=1, source_target_pairs={{0,4},{4,8},{8,12},{12,16},{16,20},{20,24},{24,28},{1,5},{5,9},{9,... | collective-permute-start | bytes 98312 | tf_op jit(solution)/shard_map/ppermute | solution.py:16
  57.7 3.5 %collective-permute-start.13 = (bf16[1,8,16,128]{3,2,1,0:T(8,128)(2,1)S(1)}, bf16[1,8,16,128]{3,2,1,0:T(8,128)(2,1)S(1)}, u32[]{:S(2)}, u32[]{:S(2)}) collective-permute-start(bf16[1,8,16,128]{3,2,1,0:T(8,128)(2,1)S(1)} %get-tuple-element.40), channel_id=1, source_target_pairs={{4,0},{8,4},{12,8},{16,12},{20,16},{24,20},{28,24},{5,1},{9,5},{13... | collective-permute-start | bytes 98312 | tf_op jit(solution)/shard_map/ppermute | solution.py:17
  61.2 1.9 %collective-permute-done.13 = bf16[1,8,16,128]{3,2,1,0:T(8,128)(2,1)S(1)} collective-permute-done((bf16[1,8,16,128]{3,2,1,0:T(8,128)(2,1)S(1)}, bf16[1,8,16,128]{3,2,1,0:T(8,128)(2,1)S(1)}, u32[]{:S(2)}, u32[]{:S(2)}) %collective-permute-start.13) | collective-permute-done | bytes 32800 | tf_op jit(solution)/shard_map/ppermute | solution.py:17
  63.1 1.3 %collective-permute-start.14 = (bf16[4,1,16,128]{3,2,1,0:T(8,128)(2,1)S(1)}, bf16[4,1,16,128]{3,2,1,0:T(8,128)(2,1)S(1)}, u32[]{:S(2)}, u32[]{:S(2)}) collective-permute-start(bf16[4,1,16,128]{3,2,1,0:T(8,128)(2,1)S(1)} %get-tuple-element.27), channel_id=1, source_target_pairs={{1,0},{2,1},{3,2},{5,4},{6,5},{7,6},{9,8},{10,9},{11,10},{13,12},{... | collective-permute-start | bytes 49160 | tf_op jit(solution)/shard_map/ppermute | solution.py:17
  64.4 4.5 %collective-permute-start.15 = (bf16[4,1,16,128]{3,2,1,0:T(8,128)(2,1)S(1)}, bf16[4,1,16,128]{3,2,1,0:T(8,128)(2,1)S(1)}, u32[]{:S(2)}, u32[]{:S(2)}) collective-permute-start(bf16[4,1,16,128]{3,2,1,0:T(8,128)(2,1)S(1)} %get-tuple-element.28), channel_id=1, source_target_pairs={{0,1},{1,2},{2,3},{4,5},{5,6},{6,7},{8,9},{9,10},{10,11},{12,13},{... | collective-permute-start | bytes 49160 | tf_op jit(solution)/shard_map/ppermute | solution.py:16
  71.5 1.3 %multiply_reduce_fusion = (f32[6,16]{1,0:T(8,128)S(1)}, f32[6,2,8,16,128]{4,3,2,1,0:T(8,128)}) fusion(f32[2,8,16,128]{3,2,1,0:T(8,128)S(1)} %multiply_subtract_fusion, f32[6]{0:T(128)S(1)} %get-tuple-element.5, f32[2,8,16,128]{3,2,1,0:T(8,128)S(1)} %get-tuple-element.12, f32[6]{0:T(128)S(1)} %get-tuple-element.6, f32[2,8,16,128]{3,2,1,0:T(8,128)S(1)} %get-tuple-element.16, ...), kind=kLoop, calls=%fused_computation | loop fusion | flops 2162592 | bytes 1442296 | tf_op jit(solution)/shard_map/reduce_sum | solution.py:88
  72.8 10.9 %psum.14 = f32[6,16]{1,0:T(8,128)S(1)} all-reduce(f32[6,16]{1,0:T(8,128)S(1)} %get-tuple-element.7), channel_id=1, replica_groups=mesh['gx'=8,'gy'=4] {'gy'}, use_global_device_ids=true, to_apply=%region_1.2 | all-reduce | flops 96 | bytes 768 | tf_op jit(solution)/shard_map/psum | solution.py:89
  83.7 16.9 %psum.15 = f32[6,16]{1,0:T(8,128)S(1)} all-reduce(f32[6,16]{1,0:T(8,128)S(1)} %psum.14), channel_id=1, replica_groups=mesh['gx'=8,'gy'=4] {'gx'}, use_global_device_ids=true, to_apply=%region_2.3 | all-reduce | flops 96 | bytes 768 | tf_op jit(solution)/shard_map/psum | solution.py:89
  (77 shorter events, 8.2 us)
Async XLA Ops:
  0.6 19.1 %copy-start = (bf16[2,8,4,128,128]{4,3,2,1,0:T(8,128)(2,1)S(1)}, bf16[2,8,4,128,128]{4,3,2,1,0:T(8,128)(2,1)}, u32[]{:S(2)}) copy-start(bf16[2,8,4,128,128]{4,3,2,1,0:T(8,128)(2,1)} %param.9) | copy-start | bytes 6291460
  3.3 8.4 %collective-permute-start = (bf16[1,8,17,128]{3,2,1,0:T(8,128)(2,1)S(1)}, bf16[1,8,17,128]{3,2,1,0:T(8,128)(2,1)S(1)}, u32[]{:S(2)}, u32[]{:S(2)}) collective-permute-start(bf16[1,8,17,128]{3,2,1,0:T(8,128)(2,1)S(1)} %get-tuple-element.37), channel_id=1, source_target_pairs={{0,4},{4,8},{8,12},{12,16},{16,20},{20,24},{24,28},{1,5},{5,9},{9,... | collective-permute-start | bytes 104456 | tf_op jit(solution)/shard_map/ppermute | solution.py:16
  7.0 5.4 %collective-permute-start.1 = (bf16[1,8,17,128]{3,2,1,0:T(8,128)(2,1)S(1)}, bf16[1,8,17,128]{3,2,1,0:T(8,128)(2,1)S(1)}, u32[]{:S(2)}, u32[]{:S(2)}) collective-permute-start(bf16[1,8,17,128]{3,2,1,0:T(8,128)(2,1)S(1)} %get-tuple-element.38), channel_id=1, source_target_pairs={{4,0},{8,4},{12,8},{16,12},{20,16},{24,20},{28,24},{5,1},{9,5},{13... | collective-permute-start | bytes 104456 | tf_op jit(solution)/shard_map/ppermute | solution.py:17
  12.4 6.0 %collective-permute-start.2 = (bf16[4,1,17,128]{3,2,1,0:T(8,128)(2,1)S(1)}, bf16[4,1,17,128]{3,2,1,0:T(8,128)(2,1)S(1)}, u32[]{:S(2)}, u32[]{:S(2)}) collective-permute-start(bf16[4,1,17,128]{3,2,1,0:T(8,128)(2,1)S(1)} %get-tuple-element.23), channel_id=1, source_target_pairs={{1,0},{2,1},{3,2},{5,4},{6,5},{7,6},{9,8},{10,9},{11,10},{13,12},{... | collective-permute-start | bytes 52232 | tf_op jit(solution)/shard_map/ppermute | solution.py:17
  13.7 4.9 %collective-permute-start.3 = (bf16[4,1,17,128]{3,2,1,0:T(8,128)(2,1)S(1)}, bf16[4,1,17,128]{3,2,1,0:T(8,128)(2,1)S(1)}, u32[]{:S(2)}, u32[]{:S(2)}) collective-permute-start(bf16[4,1,17,128]{3,2,1,0:T(8,128)(2,1)S(1)} %get-tuple-element.24), channel_id=1, source_target_pairs={{0,1},{1,2},{2,3},{4,5},{5,6},{6,7},{8,9},{9,10},{10,11},{12,13},{... | collective-permute-start | bytes 52232 | tf_op jit(solution)/shard_map/ppermute | solution.py:16
  19.5 1.0 copy-start.1
  20.6 6.0 %collective-permute-start.4 = (bf16[1,8,16,128]{3,2,1,0:T(8,128)(2,1)S(1)}, bf16[1,8,16,128]{3,2,1,0:T(8,128)(2,1)S(1)}, u32[]{:S(2)}, u32[]{:S(2)}) collective-permute-start(bf16[1,8,16,128]{3,2,1,0:T(8,128)(2,1)S(1)} %get-tuple-element.43), channel_id=1, source_target_pairs={{0,4},{4,8},{8,12},{12,16},{16,20},{20,24},{24,28},{1,5},{5,9},{9,... | collective-permute-start | bytes 98312 | tf_op jit(solution)/shard_map/ppermute | solution.py:16
  24.7 5.2 %collective-permute-start.5 = (bf16[1,8,16,128]{3,2,1,0:T(8,128)(2,1)S(1)}, bf16[1,8,16,128]{3,2,1,0:T(8,128)(2,1)S(1)}, u32[]{:S(2)}, u32[]{:S(2)}) collective-permute-start(bf16[1,8,16,128]{3,2,1,0:T(8,128)(2,1)S(1)} %get-tuple-element.44), channel_id=1, source_target_pairs={{4,0},{8,4},{12,8},{16,12},{20,16},{24,20},{28,24},{5,1},{9,5},{13... | collective-permute-start | bytes 98312 | tf_op jit(solution)/shard_map/ppermute | solution.py:17
  29.9 5.9 %collective-permute-start.6 = (bf16[4,1,16,128]{3,2,1,0:T(8,128)(2,1)S(1)}, bf16[4,1,16,128]{3,2,1,0:T(8,128)(2,1)S(1)}, u32[]{:S(2)}, u32[]{:S(2)}) collective-permute-start(bf16[4,1,16,128]{3,2,1,0:T(8,128)(2,1)S(1)} %get-tuple-element.35), channel_id=1, source_target_pairs={{1,0},{2,1},{3,2},{5,4},{6,5},{7,6},{9,8},{10,9},{11,10},{13,12},{... | collective-permute-start | bytes 49160 | tf_op jit(solution)/shard_map/ppermute | solution.py:17
  31.2 5.4 %collective-permute-start.7 = (bf16[4,1,16,128]{3,2,1,0:T(8,128)(2,1)S(1)}, bf16[4,1,16,128]{3,2,1,0:T(8,128)(2,1)S(1)}, u32[]{:S(2)}, u32[]{:S(2)}) collective-permute-start(bf16[4,1,16,128]{3,2,1,0:T(8,128)(2,1)S(1)} %get-tuple-element.36), channel_id=1, source_target_pairs={{0,1},{1,2},{2,3},{4,5},{5,6},{6,7},{8,9},{9,10},{10,11},{12,13},{... | collective-permute-start | bytes 49160 | tf_op jit(solution)/shard_map/ppermute | solution.py:16
  38.4 5.4 %collective-permute-start.8 = (bf16[1,8,16,128]{3,2,1,0:T(8,128)(2,1)S(1)}, bf16[1,8,16,128]{3,2,1,0:T(8,128)(2,1)S(1)}, u32[]{:S(2)}, u32[]{:S(2)}) collective-permute-start(bf16[1,8,16,128]{3,2,1,0:T(8,128)(2,1)S(1)} %get-tuple-element.41), channel_id=1, source_target_pairs={{0,4},{4,8},{8,12},{12,16},{16,20},{20,24},{24,28},{1,5},{5,9},{9,... | collective-permute-start | bytes 98312 | tf_op jit(solution)/shard_map/ppermute | solution.py:16
  41.2 5.2 %collective-permute-start.9 = (bf16[1,8,16,128]{3,2,1,0:T(8,128)(2,1)S(1)}, bf16[1,8,16,128]{3,2,1,0:T(8,128)(2,1)S(1)}, u32[]{:S(2)}, u32[]{:S(2)}) collective-permute-start(bf16[1,8,16,128]{3,2,1,0:T(8,128)(2,1)S(1)} %get-tuple-element.42), channel_id=1, source_target_pairs={{4,0},{8,4},{12,8},{16,12},{20,16},{24,20},{28,24},{5,1},{9,5},{13... | collective-permute-start | bytes 98312 | tf_op jit(solution)/shard_map/ppermute | solution.py:17
  46.4 5.8 %collective-permute-start.10 = (bf16[4,1,16,128]{3,2,1,0:T(8,128)(2,1)S(1)}, bf16[4,1,16,128]{3,2,1,0:T(8,128)(2,1)S(1)}, u32[]{:S(2)}, u32[]{:S(2)}) collective-permute-start(bf16[4,1,16,128]{3,2,1,0:T(8,128)(2,1)S(1)} %get-tuple-element.31), channel_id=1, source_target_pairs={{1,0},{2,1},{3,2},{5,4},{6,5},{7,6},{9,8},{10,9},{11,10},{13,12},{... | collective-permute-start | bytes 49160 | tf_op jit(solution)/shard_map/ppermute | solution.py:17
  47.7 5.4 %collective-permute-start.11 = (bf16[4,1,16,128]{3,2,1,0:T(8,128)(2,1)S(1)}, bf16[4,1,16,128]{3,2,1,0:T(8,128)(2,1)S(1)}, u32[]{:S(2)}, u32[]{:S(2)}) collective-permute-start(bf16[4,1,16,128]{3,2,1,0:T(8,128)(2,1)S(1)} %get-tuple-element.32), channel_id=1, source_target_pairs={{0,1},{1,2},{2,3},{4,5},{5,6},{6,7},{8,9},{9,10},{10,11},{12,13},{... | collective-permute-start | bytes 49160 | tf_op jit(solution)/shard_map/ppermute | solution.py:16
  53.9 15.0 %copy-start.2 = (f32[6,5]{1,0:T(8,128)S(1)}, f32[6,5]{1,0:T(8,128)}, u32[]{:S(2)}) copy-start(f32[6,5]{1,0:T(8,128)} %param.14) | copy-start | bytes 364
  54.9 6.3 %collective-permute-start.12 = (bf16[1,8,16,128]{3,2,1,0:T(8,128)(2,1)S(1)}, bf16[1,8,16,128]{3,2,1,0:T(8,128)(2,1)S(1)}, u32[]{:S(2)}, u32[]{:S(2)}) collective-permute-start(bf16[1,8,16,128]{3,2,1,0:T(8,128)(2,1)S(1)} %get-tuple-element.39), channel_id=1, source_target_pairs={{0,4},{4,8},{8,12},{12,16},{16,20},{20,24},{24,28},{1,5},{5,9},{9,... | collective-permute-start | bytes 98312 | tf_op jit(solution)/shard_map/ppermute | solution.py:16
  57.7 5.4 %collective-permute-start.13 = (bf16[1,8,16,128]{3,2,1,0:T(8,128)(2,1)S(1)}, bf16[1,8,16,128]{3,2,1,0:T(8,128)(2,1)S(1)}, u32[]{:S(2)}, u32[]{:S(2)}) collective-permute-start(bf16[1,8,16,128]{3,2,1,0:T(8,128)(2,1)S(1)} %get-tuple-element.40), channel_id=1, source_target_pairs={{4,0},{8,4},{12,8},{16,12},{20,16},{24,20},{28,24},{5,1},{9,5},{13... | collective-permute-start | bytes 98312 | tf_op jit(solution)/shard_map/ppermute | solution.py:17
  63.1 6.1 %collective-permute-start.14 = (bf16[4,1,16,128]{3,2,1,0:T(8,128)(2,1)S(1)}, bf16[4,1,16,128]{3,2,1,0:T(8,128)(2,1)S(1)}, u32[]{:S(2)}, u32[]{:S(2)}) collective-permute-start(bf16[4,1,16,128]{3,2,1,0:T(8,128)(2,1)S(1)} %get-tuple-element.27), channel_id=1, source_target_pairs={{1,0},{2,1},{3,2},{5,4},{6,5},{7,6},{9,8},{10,9},{11,10},{13,12},{... | collective-permute-start | bytes 49160 | tf_op jit(solution)/shard_map/ppermute | solution.py:17
  64.4 5.4 %collective-permute-start.15 = (bf16[4,1,16,128]{3,2,1,0:T(8,128)(2,1)S(1)}, bf16[4,1,16,128]{3,2,1,0:T(8,128)(2,1)S(1)}, u32[]{:S(2)}, u32[]{:S(2)}) collective-permute-start(bf16[4,1,16,128]{3,2,1,0:T(8,128)(2,1)S(1)} %get-tuple-element.28), channel_id=1, source_target_pairs={{0,1},{1,2},{2,3},{4,5},{5,6},{6,7},{8,9},{9,10},{10,11},{12,13},{... | collective-permute-start | bytes 49160 | tf_op jit(solution)/shard_map/ppermute | solution.py:16
